TPU v7x, 32 devices: a whole 2x2x4 slice. The times are simulated.
32 devices in a mesh: expert: 4 (over y, core), fsdp: 8 (over z, x).
Axes of the slice: x: 2, y: 2, z: 4, core: 2. Of those that a mesh axis runs over, the one named last changes fastest.
Arguments:
- gradients: bfloat16 [8, 3584, 1024], P('expert', 'fsdp'), may hold values from -24 to 24, as said below
- owner: int32 [4, 2], P('expert'), may hold values from 0 to 1, each once within a row
Outputs:
- updates: bfloat16 [8, 3584, 1024], P('expert', 'fsdp')
- slot_rms: float32 [4, 8], P('expert', 'fsdp')
Inputs may be any that keep to these rules, and one draw needn't show every extreme that they name: gradients are values of mean zero and unit variance times a factor per expert between 0.5 and 2 and a factor per expert and row slice between 0.5 and 2, each entry within 24 in magnitude. Each row of owner names every place 0 to 1 exactly once.
All inputs are finite; a program needn't handle non-finite values.
Results may differ from a plain program's by a relative error of at most 0.009.
Values may be sent and summed in bfloat16 or wider, within the bound.
A program may use at most 64 MiB of HBM per device.

v0:
```python
import math
import jax
import jax.numpy as jnp
from jax import lax
from jax.sharding import PartitionSpec as P

ROWS = 3584
COLS = 1024
SHARE = 4
ITERS = 3
coef_a = 3.4445
coef_b = -4.775
coef_c = 2.0315
epsilon = 1e-07


def as_sent(value):
    return jax.tree.map(lambda a: a.astype(jnp.bfloat16) if a.dtype == jnp.float32 else a, value)


def partner_2(value, axis, distance):
    mask = 2**distance
    pairs = [(source, source ^ mask) for source in range(lax.axis_size(axis))]
    return lax.ppermute(value, axis, pairs)


def select_half(stacked, bit_value):
    retained = lax.dynamic_index_in_dim(stacked, bit_value, 0, keepdims=False)
    outgoing = lax.dynamic_index_in_dim(stacked, 1 - bit_value, 0, keepdims=False)
    return (retained, outgoing)


def join_halves(own_block, theirs, bit_value):
    leading = jnp.where(bit_value == 0, own_block, theirs)
    trailing = jnp.where(bit_value == 0, theirs, own_block)
    return jnp.concatenate([leading, trailing], axis=0)


def reduce_gram(current, low_bit, high_bit):
    partial_gram = lax.dot_general(
        current, current, (((0,), (0,)), ((), ())), preferred_element_type=jnp.float32
    )
    rounded = lax.optimization_barrier(partial_gram.astype(jnp.bfloat16))
    columns = rounded.shape[1]
    retained, outgoing = select_half(rounded.reshape(2, columns // 2, columns), low_bit)
    arrived = partner_2(as_sent(outgoing), "fsdp", 0).astype(outgoing.dtype)
    pair_sum = retained.astype(jnp.float32) + arrived.astype(jnp.float32)
    retained_pair, outgoing_pair = select_half(pair_sum.reshape(2, columns // 4, columns), high_bit)
    arrived_pair = partner_2(as_sent(outgoing_pair), "fsdp", 1).astype(outgoing_pair.dtype)
    return (retained_pair + arrived_pair).astype(jnp.bfloat16)


def spread_gram(quarter, low_bit, high_bit):
    incoming = partner_2(quarter, "fsdp", 1)
    half_block = join_halves(quarter, incoming, high_bit)
    partner = partner_2(as_sent(half_block), "fsdp", 0).astype(half_block.dtype)
    return join_halves(half_block, partner, low_bit)


def body(gradients, owner):
    expert_count, local_rows, columns = gradients.shape
    fsdp_index = lax.axis_index("fsdp")
    low_bit = fsdp_index % 2
    high_bit = fsdp_index // 2 % 2
    owner_row = owner[0]
    places = jnp.arange(expert_count, dtype=jnp.int32)
    inverse = jnp.sum(
        jnp.where(owner_row[None, :] == places[:, None], places[None, :], 0), axis=1
    ).astype(jnp.int32)
    expert_sums = jnp.sum(jnp.square(gradients.astype(jnp.float32)), axis=(1, 2))
    totals = lax.psum(expert_sums, "fsdp")
    own_expert = lax.dynamic_index_in_dim(inverse, fsdp_index // SHARE, 0, keepdims=False)
    square_sum = lax.dynamic_index_in_dim(totals, own_expert, 0, keepdims=False)
    ordered = jnp.take(gradients, inverse, axis=0)
    outbound = ordered.reshape(expert_count * SHARE, local_rows // SHARE, columns)
    held = lax.all_to_all(outbound, "fsdp", split_axis=0, concat_axis=1, tiled=True)[0]
    norm_value = jnp.sqrt(square_sum)
    current = (held.astype(jnp.float32) / (norm_value + epsilon)).astype(jnp.bfloat16)
    for iteration in range(ITERS):
        quarter = reduce_gram(current, low_bit, high_bit)
        gram_full = spread_gram(quarter, low_bit, high_bit)
        squared = jnp.dot(gram_full, gram_full, preferred_element_type=jnp.float32)
        poly = (coef_b * gram_full.astype(jnp.float32) + coef_c * squared).astype(jnp.bfloat16)
        current = (
            coef_a * current.astype(jnp.float32)
            + jnp.dot(current, poly, preferred_element_type=jnp.float32)
        ).astype(jnp.bfloat16)
    update = (math.sqrt(ROWS) * current.astype(jnp.float32)).astype(jnp.bfloat16)
    returned = lax.all_to_all(update[None], "fsdp", split_axis=1, concat_axis=0, tiled=True)
    slot_order = returned.reshape(expert_count, local_rows, columns)
    updates = jnp.take(slot_order, owner_row, axis=0)
    slot_rms = (norm_value / math.sqrt(ROWS * COLS)).reshape(1, 1).astype(jnp.float32)
    return (updates, slot_rms)


def solution(mesh):
    placed = (P("expert", "fsdp", None), P("expert", None))
    return jax.shard_map(
        body,
        mesh=mesh,
        in_specs=placed,
        out_specs=(P("expert", "fsdp", None), P("expert", "fsdp")),
        check_vma=False,
    )
```

profile of v0, /device:TPU:0, one launch (start us, length us, event | category | flops | bytes accessed | tf_op | source)
XLA Modules:
  0.0 340.0 jit_solution(16962302694401268506)
XLA Ops:
  0.6 0.8 fusion.16
  1.4 0.7 compare_select_fusion
  2.1 0.7 compare_and_fusion
  2.7 2.2 gather_fusion
  4.9 1.5 broadcast_select_fusion.1
  6.4 7.3 %all-to-all-start = ((bf16[8,112,1024]{2,1,0:T(8,128)(2,1)}), bf16[8,112,1024]{2,1,0:T(8,128)(2,1)S(1)}, u32[]{:S(2)}, u32[]{:S(2)}) async-start(bf16[8,112,1024]{2,1,0:T(8,128)(2,1)} %bitcast.71), calls=%async_computation | async-start | bytes 3670016 | tf_op jit(solution)/shard_map/all_to_all | solution.py:76
  13.7 2.1 multiply_reduce_fusion
  15.7 43.7 %psum.7 = f32[2]{0:T(128)S(1)} all-reduce(f32[2]{0:T(128)S(1)} %multiply_reduce_fusion), channel_id=1, replica_groups=mesh['expert'=4,'fsdp'=8] {'fsdp'}, use_global_device_ids=true, to_apply=%region_2.4 | all-reduce | flops 2 | bytes 16 | tf_op jit(solution)/shard_map/psum | solution.py:71
  59.4 0.6 dynamic_slice.46
  62.0 0.6 dynamic_slice.47
  63.3 0.4 divide_convert_fusion
  63.7 2.4 bitcast_convert_fusion
  66.2 1.3 copy-done
  67.5 5.0 %collective-permute-start = (bf16[512,1024]{1,0:T(8,128)(2,1)S(1)}, bf16[512,1024]{1,0:T(8,128)(2,1)S(1)}, u32[]{:S(2)}, u32[]{:S(2)}) collective-permute-start(bf16[512,1024]{1,0:T(8,128)(2,1)S(1)} %dynamic-slice_bitcast_fusion.2), channel_id=1, source_target_pairs={{0,1},{1,0},{2,3},{3,2},{4,5},{5,4},{6,7},{7,6},{8,9},{9,8},{10,11... | collective-permute-start | bytes 3145736 | tf_op jit(solution)/shard_map/ppermute | solution.py:24
  72.6 19.5 %collective-permute-done = bf16[512,1024]{1,0:T(8,128)(2,1)S(1)} collective-permute-done((bf16[512,1024]{1,0:T(8,128)(2,1)S(1)}, bf16[512,1024]{1,0:T(8,128)(2,1)S(1)}, u32[]{:S(2)}, u32[]{:S(2)}) %collective-permute-start) | collective-permute-done | bytes 1048608 | tf_op jit(solution)/shard_map/ppermute | solution.py:24
  92.0 1.6 convert_add_fusion.2
  93.6 0.1 fusion.13
  93.7 3.4 collective-permute-start.1
  97.1 9.9 %collective-permute-done.1 = bf16[256,1024]{1,0:T(8,128)(2,1)S(1)} collective-permute-done((bf16[256,1024]{1,0:T(8,128)(2,1)S(1)}, bf16[256,1024]{1,0:T(8,128)(2,1)S(1)}, u32[]{:S(2)}, u32[]{:S(2)}) %collective-permute-start.1) | collective-permute-done | bytes 524320 | tf_op jit(solution)/shard_map/ppermute | solution.py:24
  107.0 0.1 fusion.12
  107.1 2.1 collective-permute-start.2
  109.2 7.2 %collective-permute-done.2 = bf16[256,1024]{1,0:T(8,128)(2,1)S(1)} collective-permute-done((bf16[256,1024]{1,0:T(8,128)(2,1)S(1)}, bf16[256,1024]{1,0:T(8,128)(2,1)S(1)}, u32[]{:S(2)}, u32[]{:S(2)}) %collective-permute-start.2) | collective-permute-done | bytes 524320 | tf_op jit(solution)/shard_map/ppermute | solution.py:24
  116.5 2.2 collective-permute-start.3
  118.7 18.2 %collective-permute-done.3 = bf16[512,1024]{1,0:T(8,128)(2,1)S(1)} collective-permute-done((bf16[512,1024]{1,0:T(8,128)(2,1)S(1)}, bf16[512,1024]{1,0:T(8,128)(2,1)S(1)}, u32[]{:S(2)}, u32[]{:S(2)}) %collective-permute-start.3) | collective-permute-done | bytes 1048608 | tf_op jit(solution)/shard_map/ppermute | solution.py:24
  136.8 0.5 broadcast_select_fusion.7
  137.4 2.5 add_convert_fusion.2
  139.9 2.1 add_convert_fusion.5
  141.9 2.4 convolution_convert_fusion.1
  144.4 1.8 collective-permute-start.4
  146.2 17.6 %collective-permute-done.4 = bf16[512,1024]{1,0:T(8,128)(2,1)S(1)} collective-permute-done((bf16[512,1024]{1,0:T(8,128)(2,1)S(1)}, bf16[512,1024]{1,0:T(8,128)(2,1)S(1)}, u32[]{:S(2)}, u32[]{:S(2)}) %collective-permute-start.4) | collective-permute-done | bytes 1048608 | tf_op jit(solution)/shard_map/ppermute | solution.py:24
  163.8 0.4 convert_add_fusion.1
  164.3 1.0 collective-permute-start.5
  165.3 13.1 %collective-permute-done.5 = bf16[256,1024]{1,0:T(8,128)(2,1)S(1)} collective-permute-done((bf16[256,1024]{1,0:T(8,128)(2,1)S(1)}, bf16[256,1024]{1,0:T(8,128)(2,1)S(1)}, u32[]{:S(2)}, u32[]{:S(2)}) %collective-permute-start.5) | collective-permute-done | bytes 524320 | tf_op jit(solution)/shard_map/ppermute | solution.py:24
  178.5 0.2 fusion.11
  178.6 1.5 collective-permute-start.6
  180.1 7.7 %collective-permute-done.6 = bf16[256,1024]{1,0:T(8,128)(2,1)S(1)} collective-permute-done((bf16[256,1024]{1,0:T(8,128)(2,1)S(1)}, bf16[256,1024]{1,0:T(8,128)(2,1)S(1)}, u32[]{:S(2)}, u32[]{:S(2)}) %collective-permute-start.6) | collective-permute-done | bytes 524320 | tf_op jit(solution)/shard_map/ppermute | solution.py:24
  188.0 1.8 collective-permute-start.7
  189.8 14.4 %collective-permute-done.7 = bf16[512,1024]{1,0:T(8,128)(2,1)S(1)} collective-permute-done((bf16[512,1024]{1,0:T(8,128)(2,1)S(1)}, bf16[512,1024]{1,0:T(8,128)(2,1)S(1)}, u32[]{:S(2)}, u32[]{:S(2)}) %collective-permute-start.7) | collective-permute-done | bytes 1048608 | tf_op jit(solution)/shard_map/ppermute | solution.py:24
  204.3 0.6 broadcast_select_fusion.5
  204.9 2.7 add_convert_fusion.1
  207.5 2.1 add_convert_fusion.4
  209.6 2.4 convolution_convert_fusion
  212.1 1.5 collective-permute-start.8
  213.7 13.9 %collective-permute-done.8 = bf16[512,1024]{1,0:T(8,128)(2,1)S(1)} collective-permute-done((bf16[512,1024]{1,0:T(8,128)(2,1)S(1)}, bf16[512,1024]{1,0:T(8,128)(2,1)S(1)}, u32[]{:S(2)}, u32[]{:S(2)}) %collective-permute-start.8) | collective-permute-done | bytes 1048608 | tf_op jit(solution)/shard_map/ppermute | solution.py:24
  227.5 0.4 convert_add_fusion
  228.0 0.7 collective-permute-start.9
  228.7 11.2 %collective-permute-done.9 = bf16[256,1024]{1,0:T(8,128)(2,1)S(1)} collective-permute-done((bf16[256,1024]{1,0:T(8,128)(2,1)S(1)}, bf16[256,1024]{1,0:T(8,128)(2,1)S(1)}, u32[]{:S(2)}, u32[]{:S(2)}) %collective-permute-start.9) | collective-permute-done | bytes 524320 | tf_op jit(solution)/shard_map/ppermute | solution.py:24
  239.9 0.2 fusion.10
  240.0 0.4 collective-permute-start.10
  240.4 8.9 %collective-permute-done.10 = bf16[256,1024]{1,0:T(8,128)(2,1)S(1)} collective-permute-done((bf16[256,1024]{1,0:T(8,128)(2,1)S(1)}, bf16[256,1024]{1,0:T(8,128)(2,1)S(1)}, u32[]{:S(2)}, u32[]{:S(2)}) %collective-permute-start.10) | collective-permute-done | bytes 524320 | tf_op jit(solution)/shard_map/ppermute | solution.py:24
  249.4 1.0 collective-permute-start.11
  250.4 13.9 %collective-permute-done.11 = bf16[512,1024]{1,0:T(8,128)(2,1)S(1)} collective-permute-done((bf16[512,1024]{1,0:T(8,128)(2,1)S(1)}, bf16[512,1024]{1,0:T(8,128)(2,1)S(1)}, u32[]{:S(2)}, u32[]{:S(2)}) %collective-permute-start.11) | collective-permute-done | bytes 1048608 | tf_op jit(solution)/shard_map/ppermute | solution.py:24
  264.3 1.5 broadcast_select_fusion.3
  265.9 7.5 %fusion.9 = bf16[1,896,1024]{2,1,0:T(8,128)(2,1)S(1)} fusion(bf16[896,1024]{1,0:T(8,128)(2,1)} %copy-done.3, bf16[512,1024]{1,0:T(8,128)(2,1)} %get-tuple-element.4, bf16[512,1024]{1,0:T(8,128)(2,1)S(1)} %get-tuple-element.3), kind=kOutput, calls=%fused_computation.26 | convolution fusion | flops 4045537280 | bytes 5767168 | tf_op jit(solution)/shard_map/dot_general | solution.py:86
  273.4 4.8 %copy.9 = bf16[1,896,1024]{2,0,1:T(2,128)(2,1)} copy(bf16[1,896,1024]{2,1,0:T(8,128)(2,1)S(1)} %fusion.9) | data formatting | bytes 3670016 | tf_op jit(solution)/shard_map/broadcast_in_dim | solution.py:89
  278.2 0.5 broadcast.84
  278.7 11.4 %reduce = bf16[896,1024]{1,0:T(8,128)(2,1)S(1)} reduce(bf16[896,1,1024]{2,1,0:T(2,128)(2,1)} %bitcast.69, bf16[]{:T(256)} %broadcast.84), dimensions={1}, to_apply=%bitcast.68.reduce_sub_computation | reduce | bytes 3670018
  290.1 3.7 %reshape.106 = bf16[8,2,57344]{2,1,0:T(2,128)(2,1)} reshape(bf16[896,1024]{1,0:T(8,128)(2,1)S(1)} %reduce) | data formatting | bytes 3670016
  293.8 3.6 %all-to-all-start.1 = ((bf16[8,2,57344]{2,1,0:T(2,128)(2,1)}), bf16[8,2,57344]{2,1,0:T(2,128)(2,1)S(1)}, u32[]{:S(2)}, u32[]{:S(2)}) async-start(bf16[8,2,57344]{2,1,0:T(2,128)(2,1)} %reshape.106), calls=%async_computation.1 | async-start | bytes 3670016 | tf_op jit(solution)/shard_map/all_to_all | solution.py:89
  297.4 29.7 %all-to-all-done.1 = bf16[8,2,57344]{2,1,0:T(2,128)(2,1)S(1)} async-done(((bf16[8,2,57344]{2,1,0:T(2,128)(2,1)}), bf16[8,2,57344]{2,1,0:T(2,128)(2,1)S(1)}, u32[]{:S(2)}, u32[]{:S(2)}) %all-to-all-start.1) | async-done | bytes 1835040 | tf_op jit(solution)/shard_map/all_to_all | solution.py:89
  327.1 4.1 %reshape.107 = bf16[896,1,1024]{2,1,0:T(2,128)(2,1)} reshape(bf16[8,2,57344]{2,1,0:T(2,128)(2,1)S(1)} %all-to-all-done.1) | data formatting | bytes 3670016
  331.2 4.0 %copy.7 = bf16[1,896,1024]{2,1,0:T(8,128)(2,1)} copy(bf16[1,896,1024]{2,0,1:T(2,128)(2,1)} %bitcast.70) | data formatting | bytes 3670016
  335.2 2.2 gather_fusion.1
  337.4 1.5 broadcast_select_fusion
  (21 shorter events, 0.8 us)
Async XLA Ops:
  6.4 56.9 %all-to-all-start = ((bf16[8,112,1024]{2,1,0:T(8,128)(2,1)}), bf16[8,112,1024]{2,1,0:T(8,128)(2,1)S(1)}, u32[]{:S(2)}, u32[]{:S(2)}) async-start(bf16[8,112,1024]{2,1,0:T(8,128)(2,1)} %bitcast.71), calls=%async_computation | async-start | bytes 3670016 | tf_op jit(solution)/shard_map/all_to_all | solution.py:76
  63.7 2.4 copy-start.1
  66.1 1.3 copy-start
  67.5 24.5 %collective-permute-start = (bf16[512,1024]{1,0:T(8,128)(2,1)S(1)}, bf16[512,1024]{1,0:T(8,128)(2,1)S(1)}, u32[]{:S(2)}, u32[]{:S(2)}) collective-permute-start(bf16[512,1024]{1,0:T(8,128)(2,1)S(1)} %dynamic-slice_bitcast_fusion.2), channel_id=1, source_target_pairs={{0,1},{1,0},{2,3},{3,2},{4,5},{5,4},{6,7},{7,6},{8,9},{9,8},{10,11... | collective-permute-start | bytes 3145736 | tf_op jit(solution)/shard_map/ppermute | solution.py:24
  93.7 13.2 %collective-permute-start.1 = (bf16[256,1024]{1,0:T(8,128)(2,1)S(1)}, bf16[256,1024]{1,0:T(8,128)(2,1)S(1)}, u32[]{:S(2)}, u32[]{:S(2)}) collective-permute-start(bf16[256,1024]{1,0:T(8,128)(2,1)S(1)} %fusion.13), channel_id=1, source_target_pairs={{0,2},{1,3},{2,0},{3,1},{4,6},{5,7},{6,4},{7,5},{8,10},{9,11},{10,... | collective-permute-start | bytes 1572872 | tf_op jit(solution)/shard_map/ppermute | solution.py:24
  107.1 9.2 %collective-permute-start.2 = (bf16[256,1024]{1,0:T(8,128)(2,1)S(1)}, bf16[256,1024]{1,0:T(8,128)(2,1)S(1)}, u32[]{:S(2)}, u32[]{:S(2)}) collective-permute-start(bf16[256,1024]{1,0:T(8,128)(2,1)S(1)} %fusion.12), channel_id=1, source_target_pairs={{0,2},{1,3},{2,0},{3,1},{4,6},{5,7},{6,4},{7,5},{8,10},{9,11},{10,... | collective-permute-start | bytes 1572872 | tf_op jit(solution)/shard_map/ppermute | solution.py:24
  116.5 20.3 %collective-permute-start.3 = (bf16[512,1024]{1,0:T(8,128)(2,1)S(1)}, bf16[512,1024]{1,0:T(8,128)(2,1)S(1)}, u32[]{:S(2)}, u32[]{:S(2)}) collective-permute-start(bf16[512,1024]{1,0:T(8,128)(2,1)S(1)} %pad_maximum_fusion), channel_id=1, source_target_pairs={{0,1},{1,0},{2,3},{3,2},{4,5},{5,4},{6,7},{7,6},{8,9},{9,8},{10,11... | collective-permute-start | bytes 3145736 | tf_op jit(solution)/shard_map/ppermute | solution.py:24
  137.4 2.5 copy-start.2
  144.4 19.4 %collective-permute-start.4 = (bf16[512,1024]{1,0:T(8,128)(2,1)S(1)}, bf16[512,1024]{1,0:T(8,128)(2,1)S(1)}, u32[]{:S(2)}, u32[]{:S(2)}) collective-permute-start(bf16[512,1024]{1,0:T(8,128)(2,1)S(1)} %dynamic-slice_bitcast_fusion.1), channel_id=1, source_target_pairs={{0,1},{1,0},{2,3},{3,2},{4,5},{5,4},{6,7},{7,6},{8,9},{9,8},{10,11... | collective-permute-start | bytes 3145736 | tf_op jit(solution)/shard_map/ppermute | solution.py:24
  164.3 14.1 %collective-permute-start.5 = (bf16[256,1024]{1,0:T(8,128)(2,1)S(1)}, bf16[256,1024]{1,0:T(8,128)(2,1)S(1)}, u32[]{:S(2)}, u32[]{:S(2)}) collective-permute-start(bf16[256,1024]{1,0:T(8,128)(2,1)S(1)} %fusion.14), channel_id=1, source_target_pairs={{0,2},{1,3},{2,0},{3,1},{4,6},{5,7},{6,4},{7,5},{8,10},{9,11},{10,... | collective-permute-start | bytes 1572872 | tf_op jit(solution)/shard_map/ppermute | solution.py:24
  178.6 9.2 %collective-permute-start.6 = (bf16[256,1024]{1,0:T(8,128)(2,1)S(1)}, bf16[256,1024]{1,0:T(8,128)(2,1)S(1)}, u32[]{:S(2)}, u32[]{:S(2)}) collective-permute-start(bf16[256,1024]{1,0:T(8,128)(2,1)S(1)} %fusion.11), channel_id=1, source_target_pairs={{0,2},{1,3},{2,0},{3,1},{4,6},{5,7},{6,4},{7,5},{8,10},{9,11},{10,... | collective-permute-start | bytes 1572872 | tf_op jit(solution)/shard_map/ppermute | solution.py:24
  188.0 16.3 %collective-permute-start.7 = (bf16[512,1024]{1,0:T(8,128)(2,1)S(1)}, bf16[512,1024]{1,0:T(8,128)(2,1)S(1)}, u32[]{:S(2)}, u32[]{:S(2)}) collective-permute-start(bf16[512,1024]{1,0:T(8,128)(2,1)S(1)} %pad_maximum_fusion.1), channel_id=1, source_target_pairs={{0,1},{1,0},{2,3},{3,2},{4,5},{5,4},{6,7},{7,6},{8,9},{9,8},{10,11... | collective-permute-start | bytes 3145736 | tf_op jit(solution)/shard_map/ppermute | solution.py:24
  209.6 2.4 copy-start.3
  212.1 15.4 %collective-permute-start.8 = (bf16[512,1024]{1,0:T(8,128)(2,1)S(1)}, bf16[512,1024]{1,0:T(8,128)(2,1)S(1)}, u32[]{:S(2)}, u32[]{:S(2)}) collective-permute-start(bf16[512,1024]{1,0:T(8,128)(2,1)S(1)} %dynamic-slice_bitcast_fusion), channel_id=1, source_target_pairs={{0,1},{1,0},{2,3},{3,2},{4,5},{5,4},{6,7},{7,6},{8,9},{9,8},{10,11... | collective-permute-start | bytes 3145736 | tf_op jit(solution)/shard_map/ppermute | solution.py:24
  228.0 11.9 %collective-permute-start.9 = (bf16[256,1024]{1,0:T(8,128)(2,1)S(1)}, bf16[256,1024]{1,0:T(8,128)(2,1)S(1)}, u32[]{:S(2)}, u32[]{:S(2)}) collective-permute-start(bf16[256,1024]{1,0:T(8,128)(2,1)S(1)} %fusion.15), channel_id=1, source_target_pairs={{0,2},{1,3},{2,0},{3,1},{4,6},{5,7},{6,4},{7,5},{8,10},{9,11},{10,... | collective-permute-start | bytes 1572872 | tf_op jit(solution)/shard_map/ppermute | solution.py:24
  240.0 9.2 %collective-permute-start.10 = (bf16[256,1024]{1,0:T(8,128)(2,1)S(1)}, bf16[256,1024]{1,0:T(8,128)(2,1)S(1)}, u32[]{:S(2)}, u32[]{:S(2)}) collective-permute-start(bf16[256,1024]{1,0:T(8,128)(2,1)S(1)} %fusion.10), channel_id=1, source_target_pairs={{0,2},{1,3},{2,0},{3,1},{4,6},{5,7},{6,4},{7,5},{8,10},{9,11},{10,... | collective-permute-start | bytes 1572872 | tf_op jit(solution)/shard_map/ppermute | solution.py:24
  249.4 14.9 %collective-permute-start.11 = (bf16[512,1024]{1,0:T(8,128)(2,1)S(1)}, bf16[512,1024]{1,0:T(8,128)(2,1)S(1)}, u32[]{:S(2)}, u32[]{:S(2)}) collective-permute-start(bf16[512,1024]{1,0:T(8,128)(2,1)S(1)} %pad_maximum_fusion.2), channel_id=1, source_target_pairs={{0,1},{1,0},{2,3},{3,2},{4,5},{5,4},{6,7},{7,6},{8,9},{9,8},{10,11... | collective-permute-start | bytes 3145736 | tf_op jit(solution)/shard_map/ppermute | solution.py:24
  293.8 33.3 %all-to-all-start.1 = ((bf16[8,2,57344]{2,1,0:T(2,128)(2,1)}), bf16[8,2,57344]{2,1,0:T(2,128)(2,1)S(1)}, u32[]{:S(2)}, u32[]{:S(2)}) async-start(bf16[8,2,57344]{2,1,0:T(2,128)(2,1)} %reshape.106), calls=%async_computation.1 | async-start | bytes 3670016 | tf_op jit(solution)/shard_map/all_to_all | solution.py:89
where the time goes:
time: 341 us; the launch traced here: 340 us
  waiting for transfers between devices  185 us (54%)
  blocking collectives  43.7 us (13%)
  starting transfers between devices  33.2 us (10%)
  other arithmetic  24.9 us (7%)
  local copies, waits for them, and re-layouts  24.4 us (7%)
  matrix products  24 us (7%)
  between operations  4.74 us (1%)
    ppermute x12, waiting for transfers between devices, partner_2(): return lax.ppermute(value, axis, pairs)  155 us
    psum x1, blocking collectives, body(): totals = lax.psum(expert_sums, 'fsdp')  43.7 us
    all_to_all x1, waiting for transfers between devices, body(): lax.all_to_all(update[None], 'fsdp', split_axis=1, concat_axis=0, tiled=T...  29.7 us
    ppermute x12, starting transfers between devices, partner_2(): return lax.ppermute(value, axis, pairs)  22.3 us
    unnamed x12, local copies, waits for them, and re-layouts  13.6 us
    dot_general x3, matrix products, body(): jnp.dot(current, poly, preferred_element_type=jnp.float32)  11.7 us
    unnamed x1, other arithmetic  11.4 us
    all_to_all x1, starting transfers between devices, body(): lax.all_to_all(outbound, 'fsdp', split_axis=0, concat_axis=1, tiled=True)[0]  7.28 us
  transfers between devices with their start and end apart: 14, of which 13 were waited for; matrix products, arithmetic and copies ran while one was open for 1% of the time, Pallas kernels for 0%

commit v1 on v0

--- a/solution.py
+++ b/solution.py
@@ -86,7 +86,12 @@
             + jnp.dot(current, poly, preferred_element_type=jnp.float32)
         ).astype(jnp.bfloat16)
     update = (math.sqrt(ROWS) * current.astype(jnp.float32)).astype(jnp.bfloat16)
-    returned = lax.all_to_all(update[None], "fsdp", split_axis=1, concat_axis=0, tiled=True)
+    returned = jnp.concatenate(
+        lax.all_to_all(
+            jnp.stack(jnp.split(update[None], lax.axis_size("fsdp"), axis=1)), "fsdp", 0, 0
+        ),
+        axis=0,
+    )
     slot_order = returned.reshape(expert_count, local_rows, columns)
     updates = jnp.take(slot_order, owner_row, axis=0)
     slot_rms = (norm_value / math.sqrt(ROWS * COLS)).reshape(1, 1).astype(jnp.float32)

time: 341 us -> 318 us (0.933)
  local copies, waits for them, and re-layouts: 24.4 us -> 12.7 us
  other arithmetic: 24.9 us -> 13.7 us
    unnamed x1 -> x0, other arithmetic: 11.4 us -> none
    unnamed x12 -> x17, local copies, waits for them, and re-layouts: 13.6 us -> 6.28 us
    broadcast_in_dim x1 -> x0, local copies, waits for them, and re-layouts: 4.84 us -> none  [body(): update[None]]
where the time goes in v1:
time: 318 us; the launch traced here: 317 us
  waiting for transfers between devices  185 us (58%)
  blocking collectives  43.7 us (14%)
  starting transfers between devices  33.2 us (10%)
  matrix products  24.2 us (8%)
  other arithmetic  13.7 us (4%)
  local copies, waits for them, and re-layouts  12.7 us (4%)
  between operations  4.76 us (1%)
    ppermute x12, waiting for transfers between devices, partner_2(): return lax.ppermute(value, axis, pairs)  155 us
    psum x1, blocking collectives, body(): totals = lax.psum(expert_sums, 'fsdp')  43.7 us
    all_to_all x1, waiting for transfers between devices, body(): lax.all_to_all(jnp.stack(jnp.split(update[None], lax.axis_size('fsdp'), a...  29.7 us
    ppermute x12, starting transfers between devices, partner_2(): return lax.ppermute(value, axis, pairs)  22.4 us
    dot_general x3, matrix products, body(): jnp.dot(current, poly, preferred_element_type=jnp.float32)  11.8 us
    all_to_all x1, starting transfers between devices, body(): lax.all_to_all(outbound, 'fsdp', split_axis=0, concat_axis=1, tiled=True)[0]  7.28 us
    dot_general x3, matrix products, reduce_gram(): lax.dot_general(current, current, (((0,), (0,)), ((), ())), preferred_ele...  7.18 us
  transfers between devices with their start and end apart: 14, of which 13 were waited for; matrix products, arithmetic and copies ran while one was open for 1% of the time, Pallas kernels for 0%

profile of v1, /device:TPU:0, one launch (start us, length us, event | category | flops | bytes accessed | tf_op | source)
XLA Modules:
  0.0 317.1 jit_solution(306512624130062416)
XLA Ops:
  0.6 0.8 fusion.24
  1.4 2.2 gather_fusion
  3.6 1.5 broadcast_select_fusion.1
  5.1 7.3 %all-to-all-start = ((bf16[8,112,1024]{2,1,0:T(8,128)(2,1)}), bf16[8,112,1024]{2,1,0:T(8,128)(2,1)S(1)}, u32[]{:S(2)}, u32[]{:S(2)}) async-start(bf16[8,112,1024]{2,1,0:T(8,128)(2,1)} %bitcast.97), calls=%async_computation | async-start | bytes 3670016 | tf_op jit(solution)/shard_map/all_to_all | solution.py:76
  12.4 2.1 multiply_reduce_fusion
  14.4 43.7 %psum.7 = f32[2]{0:T(128)S(1)} all-reduce(f32[2]{0:T(128)S(1)} %multiply_reduce_fusion), channel_id=1, replica_groups=mesh['expert'=4,'fsdp'=8] {'fsdp'}, use_global_device_ids=true, to_apply=%region_2.4 | all-reduce | flops 2 | bytes 16 | tf_op jit(solution)/shard_map/psum | solution.py:71
  58.1 0.6 dynamic_slice.46
  60.7 0.6 dynamic_slice.47
  62.0 0.4 divide_convert_fusion
  62.4 2.4 bitcast_convert_fusion
  64.8 1.3 copy-done
  66.3 5.0 %collective-permute-start = (bf16[512,1024]{1,0:T(8,128)(2,1)S(1)}, bf16[512,1024]{1,0:T(8,128)(2,1)S(1)}, u32[]{:S(2)}, u32[]{:S(2)}) collective-permute-start(bf16[512,1024]{1,0:T(8,128)(2,1)S(1)} %dynamic-slice_bitcast_fusion.2), channel_id=1, source_target_pairs={{0,1},{1,0},{2,3},{3,2},{4,5},{5,4},{6,7},{7,6},{8,9},{9,8},{10,11... | collective-permute-start | bytes 3145736 | tf_op jit(solution)/shard_map/ppermute | solution.py:24
  71.3 19.5 %collective-permute-done = bf16[512,1024]{1,0:T(8,128)(2,1)S(1)} collective-permute-done((bf16[512,1024]{1,0:T(8,128)(2,1)S(1)}, bf16[512,1024]{1,0:T(8,128)(2,1)S(1)}, u32[]{:S(2)}, u32[]{:S(2)}) %collective-permute-start) | collective-permute-done | bytes 1048608 | tf_op jit(solution)/shard_map/ppermute | solution.py:24
  90.7 1.6 convert_add_fusion.2
  92.3 0.1 fusion.13
  92.4 3.4 %collective-permute-start.1 = (bf16[256,1024]{1,0:T(8,128)(2,1)S(1)}, bf16[256,1024]{1,0:T(8,128)(2,1)S(1)}, u32[]{:S(2)}, u32[]{:S(2)}) collective-permute-start(bf16[256,1024]{1,0:T(8,128)(2,1)S(1)} %fusion.13), channel_id=1, source_target_pairs={{0,2},{1,3},{2,0},{3,1},{4,6},{5,7},{6,4},{7,5},{8,10},{9,11},{10,... | collective-permute-start | bytes 1572872 | tf_op jit(solution)/shard_map/ppermute | solution.py:24
  95.8 9.9 %collective-permute-done.1 = bf16[256,1024]{1,0:T(8,128)(2,1)S(1)} collective-permute-done((bf16[256,1024]{1,0:T(8,128)(2,1)S(1)}, bf16[256,1024]{1,0:T(8,128)(2,1)S(1)}, u32[]{:S(2)}, u32[]{:S(2)}) %collective-permute-start.1) | collective-permute-done | bytes 524320 | tf_op jit(solution)/shard_map/ppermute | solution.py:24
  105.7 0.1 fusion.12
  105.8 2.1 collective-permute-start.2
  107.9 7.2 %collective-permute-done.2 = bf16[256,1024]{1,0:T(8,128)(2,1)S(1)} collective-permute-done((bf16[256,1024]{1,0:T(8,128)(2,1)S(1)}, bf16[256,1024]{1,0:T(8,128)(2,1)S(1)}, u32[]{:S(2)}, u32[]{:S(2)}) %collective-permute-start.2) | collective-permute-done | bytes 524320 | tf_op jit(solution)/shard_map/ppermute | solution.py:24
  115.2 2.1 collective-permute-start.3
  117.4 18.2 %collective-permute-done.3 = bf16[512,1024]{1,0:T(8,128)(2,1)S(1)} collective-permute-done((bf16[512,1024]{1,0:T(8,128)(2,1)S(1)}, bf16[512,1024]{1,0:T(8,128)(2,1)S(1)}, u32[]{:S(2)}, u32[]{:S(2)}) %collective-permute-start.3) | collective-permute-done | bytes 1048608 | tf_op jit(solution)/shard_map/ppermute | solution.py:24
  135.5 0.5 broadcast_select_fusion.7
  136.1 2.5 add_convert_fusion.2
  138.6 2.1 add_convert_fusion.5
  140.6 2.4 convolution_convert_fusion.1
  143.1 1.8 collective-permute-start.4
  144.9 17.6 %collective-permute-done.4 = bf16[512,1024]{1,0:T(8,128)(2,1)S(1)} collective-permute-done((bf16[512,1024]{1,0:T(8,128)(2,1)S(1)}, bf16[512,1024]{1,0:T(8,128)(2,1)S(1)}, u32[]{:S(2)}, u32[]{:S(2)}) %collective-permute-start.4) | collective-permute-done | bytes 1048608 | tf_op jit(solution)/shard_map/ppermute | solution.py:24
  162.5 0.4 convert_add_fusion.1
  163.0 1.0 collective-permute-start.5
  164.0 13.1 %collective-permute-done.5 = bf16[256,1024]{1,0:T(8,128)(2,1)S(1)} collective-permute-done((bf16[256,1024]{1,0:T(8,128)(2,1)S(1)}, bf16[256,1024]{1,0:T(8,128)(2,1)S(1)}, u32[]{:S(2)}, u32[]{:S(2)}) %collective-permute-start.5) | collective-permute-done | bytes 524320 | tf_op jit(solution)/shard_map/ppermute | solution.py:24
  177.2 0.2 fusion.11
  177.3 1.5 collective-permute-start.6
  178.9 7.7 %collective-permute-done.6 = bf16[256,1024]{1,0:T(8,128)(2,1)S(1)} collective-permute-done((bf16[256,1024]{1,0:T(8,128)(2,1)S(1)}, bf16[256,1024]{1,0:T(8,128)(2,1)S(1)}, u32[]{:S(2)}, u32[]{:S(2)}) %collective-permute-start.6) | collective-permute-done | bytes 524320 | tf_op jit(solution)/shard_map/ppermute | solution.py:24
  186.7 1.8 collective-permute-start.7
  188.5 14.4 %collective-permute-done.7 = bf16[512,1024]{1,0:T(8,128)(2,1)S(1)} collective-permute-done((bf16[512,1024]{1,0:T(8,128)(2,1)S(1)}, bf16[512,1024]{1,0:T(8,128)(2,1)S(1)}, u32[]{:S(2)}, u32[]{:S(2)}) %collective-permute-start.7) | collective-permute-done | bytes 1048608 | tf_op jit(solution)/shard_map/ppermute | solution.py:24
  203.0 0.6 broadcast_select_fusion.5
  203.5 2.7 add_convert_fusion.1
  206.2 2.1 add_convert_fusion.4
  208.3 2.4 convolution_convert_fusion
  210.8 1.5 collective-permute-start.8
  212.3 13.9 %collective-permute-done.8 = bf16[512,1024]{1,0:T(8,128)(2,1)S(1)} collective-permute-done((bf16[512,1024]{1,0:T(8,128)(2,1)S(1)}, bf16[512,1024]{1,0:T(8,128)(2,1)S(1)}, u32[]{:S(2)}, u32[]{:S(2)}) %collective-permute-start.8) | collective-permute-done | bytes 1048608 | tf_op jit(solution)/shard_map/ppermute | solution.py:24
  226.2 0.4 convert_add_fusion
  226.7 0.7 collective-permute-start.9
  227.4 11.1 %collective-permute-done.9 = bf16[256,1024]{1,0:T(8,128)(2,1)S(1)} collective-permute-done((bf16[256,1024]{1,0:T(8,128)(2,1)S(1)}, bf16[256,1024]{1,0:T(8,128)(2,1)S(1)}, u32[]{:S(2)}, u32[]{:S(2)}) %collective-permute-start.9) | collective-permute-done | bytes 524320 | tf_op jit(solution)/shard_map/ppermute | solution.py:24
  238.5 0.2 fusion.10
  238.7 0.4 collective-permute-start.10
  239.1 8.9 %collective-permute-done.10 = bf16[256,1024]{1,0:T(8,128)(2,1)S(1)} collective-permute-done((bf16[256,1024]{1,0:T(8,128)(2,1)S(1)}, bf16[256,1024]{1,0:T(8,128)(2,1)S(1)}, u32[]{:S(2)}, u32[]{:S(2)}) %collective-permute-start.10) | collective-permute-done | bytes 524320 | tf_op jit(solution)/shard_map/ppermute | solution.py:24
  248.1 1.0 collective-permute-start.11
  249.1 13.9 %collective-permute-done.11 = bf16[512,1024]{1,0:T(8,128)(2,1)S(1)} collective-permute-done((bf16[512,1024]{1,0:T(8,128)(2,1)S(1)}, bf16[512,1024]{1,0:T(8,128)(2,1)S(1)}, u32[]{:S(2)}, u32[]{:S(2)}) %collective-permute-start.11) | collective-permute-done | bytes 1048608 | tf_op jit(solution)/shard_map/ppermute | solution.py:24
  263.0 1.6 broadcast_select_fusion.3
  264.5 7.7 %fusion.9 = bf16[1,896,1024]{2,1,0:T(8,128)(2,1)S(1)} fusion(bf16[896,1024]{1,0:T(8,128)(2,1)} %copy-done.4, bf16[512,1024]{1,0:T(8,128)(2,1)} %get-tuple-element.4, bf16[512,1024]{1,0:T(8,128)(2,1)S(1)} %get-tuple-element.3), kind=kOutput, calls=%fused_computation.26 | convolution fusion | flops 4045537280 | bytes 5767168 | tf_op jit(solution)/shard_map/dot_general | solution.py:86
  272.2 0.7 fusion.23
  272.9 0.7 fusion.22
  273.6 0.7 fusion.21
  274.3 0.7 fusion.20
  275.0 0.7 fusion.19
  275.7 0.7 fusion.18
  276.4 0.7 fusion.17
  277.1 0.7 fusion.16
  277.8 3.6 %all-to-all-start.1 = ((bf16[8,1,112,1024]{3,2,1,0:T(8,128)(2,1)}), bf16[8,1,112,1024]{3,2,1,0:T(8,128)(2,1)S(1)}, u32[]{:S(2)}, u32[]{:S(2)}) async-start(bf16[8,1,112,1024]{3,2,1,0:T(8,128)(2,1)} %fusion.16), calls=%async_computation.1 | async-start | bytes 3670016 | tf_op jit(solution)/shard_map/all_to_all | solution.py:90
  281.5 29.7 %all-to-all-done.1 = bf16[8,1,112,1024]{3,2,1,0:T(8,128)(2,1)S(1)} async-done(((bf16[8,1,112,1024]{3,2,1,0:T(8,128)(2,1)}), bf16[8,1,112,1024]{3,2,1,0:T(8,128)(2,1)S(1)}, u32[]{:S(2)}, u32[]{:S(2)}) %all-to-all-start.1) | async-done | bytes 1835040 | tf_op jit(solution)/shard_map/all_to_all | solution.py:90
  311.2 1.9 gather_fusion.1
  313.0 3.0 broadcast_select_fusion
  (27 shorter events, 0.9 us)
Async XLA Ops:
  5.1 56.9 %all-to-all-start = ((bf16[8,112,1024]{2,1,0:T(8,128)(2,1)}), bf16[8,112,1024]{2,1,0:T(8,128)(2,1)S(1)}, u32[]{:S(2)}, u32[]{:S(2)}) async-start(bf16[8,112,1024]{2,1,0:T(8,128)(2,1)} %bitcast.97), calls=%async_computation | async-start | bytes 3670016 | tf_op jit(solution)/shard_map/all_to_all | solution.py:76
  62.4 2.4 copy-start.1
  64.8 1.3 copy-start
  66.3 24.5 %collective-permute-start = (bf16[512,1024]{1,0:T(8,128)(2,1)S(1)}, bf16[512,1024]{1,0:T(8,128)(2,1)S(1)}, u32[]{:S(2)}, u32[]{:S(2)}) collective-permute-start(bf16[512,1024]{1,0:T(8,128)(2,1)S(1)} %dynamic-slice_bitcast_fusion.2), channel_id=1, source_target_pairs={{0,1},{1,0},{2,3},{3,2},{4,5},{5,4},{6,7},{7,6},{8,9},{9,8},{10,11... | collective-permute-start | bytes 3145736 | tf_op jit(solution)/shard_map/ppermute | solution.py:24
  92.4 13.2 %collective-permute-start.1 = (bf16[256,1024]{1,0:T(8,128)(2,1)S(1)}, bf16[256,1024]{1,0:T(8,128)(2,1)S(1)}, u32[]{:S(2)}, u32[]{:S(2)}) collective-permute-start(bf16[256,1024]{1,0:T(8,128)(2,1)S(1)} %fusion.13), channel_id=1, source_target_pairs={{0,2},{1,3},{2,0},{3,1},{4,6},{5,7},{6,4},{7,5},{8,10},{9,11},{10,... | collective-permute-start | bytes 1572872 | tf_op jit(solution)/shard_map/ppermute | solution.py:24
  105.8 9.2 %collective-permute-start.2 = (bf16[256,1024]{1,0:T(8,128)(2,1)S(1)}, bf16[256,1024]{1,0:T(8,128)(2,1)S(1)}, u32[]{:S(2)}, u32[]{:S(2)}) collective-permute-start(bf16[256,1024]{1,0:T(8,128)(2,1)S(1)} %fusion.12), channel_id=1, source_target_pairs={{0,2},{1,3},{2,0},{3,1},{4,6},{5,7},{6,4},{7,5},{8,10},{9,11},{10,... | collective-permute-start | bytes 1572872 | tf_op jit(solution)/shard_map/ppermute | solution.py:24
  115.2 20.3 %collective-permute-start.3 = (bf16[512,1024]{1,0:T(8,128)(2,1)S(1)}, bf16[512,1024]{1,0:T(8,128)(2,1)S(1)}, u32[]{:S(2)}, u32[]{:S(2)}) collective-permute-start(bf16[512,1024]{1,0:T(8,128)(2,1)S(1)} %pad_maximum_fusion), channel_id=1, source_target_pairs={{0,1},{1,0},{2,3},{3,2},{4,5},{5,4},{6,7},{7,6},{8,9},{9,8},{10,11... | collective-permute-start | bytes 3145736 | tf_op jit(solution)/shard_map/ppermute | solution.py:24
  136.1 2.5 copy-start.2
  143.1 19.4 %collective-permute-start.4 = (bf16[512,1024]{1,0:T(8,128)(2,1)S(1)}, bf16[512,1024]{1,0:T(8,128)(2,1)S(1)}, u32[]{:S(2)}, u32[]{:S(2)}) collective-permute-start(bf16[512,1024]{1,0:T(8,128)(2,1)S(1)} %dynamic-slice_bitcast_fusion.1), channel_id=1, source_target_pairs={{0,1},{1,0},{2,3},{3,2},{4,5},{5,4},{6,7},{7,6},{8,9},{9,8},{10,11... | collective-permute-start | bytes 3145736 | tf_op jit(solution)/shard_map/ppermute | solution.py:24
  163.0 14.2 %collective-permute-start.5 = (bf16[256,1024]{1,0:T(8,128)(2,1)S(1)}, bf16[256,1024]{1,0:T(8,128)(2,1)S(1)}, u32[]{:S(2)}, u32[]{:S(2)}) collective-permute-start(bf16[256,1024]{1,0:T(8,128)(2,1)S(1)} %fusion.14), channel_id=1, source_target_pairs={{0,2},{1,3},{2,0},{3,1},{4,6},{5,7},{6,4},{7,5},{8,10},{9,11},{10,... | collective-permute-start | bytes 1572872 | tf_op jit(solution)/shard_map/ppermute | solution.py:24
  177.3 9.2 %collective-permute-start.6 = (bf16[256,1024]{1,0:T(8,128)(2,1)S(1)}, bf16[256,1024]{1,0:T(8,128)(2,1)S(1)}, u32[]{:S(2)}, u32[]{:S(2)}) collective-permute-start(bf16[256,1024]{1,0:T(8,128)(2,1)S(1)} %fusion.11), channel_id=1, source_target_pairs={{0,2},{1,3},{2,0},{3,1},{4,6},{5,7},{6,4},{7,5},{8,10},{9,11},{10,... | collective-permute-start | bytes 1572872 | tf_op jit(solution)/shard_map/ppermute | solution.py:24
  186.7 16.2 %collective-permute-start.7 = (bf16[512,1024]{1,0:T(8,128)(2,1)S(1)}, bf16[512,1024]{1,0:T(8,128)(2,1)S(1)}, u32[]{:S(2)}, u32[]{:S(2)}) collective-permute-start(bf16[512,1024]{1,0:T(8,128)(2,1)S(1)} %pad_maximum_fusion.1), channel_id=1, source_target_pairs={{0,1},{1,0},{2,3},{3,2},{4,5},{5,4},{6,7},{7,6},{8,9},{9,8},{10,11... | collective-permute-start | bytes 3145736 | tf_op jit(solution)/shard_map/ppermute | solution.py:24
  208.3 2.4 copy-start.4
  210.8 15.4 %collective-permute-start.8 = (bf16[512,1024]{1,0:T(8,128)(2,1)S(1)}, bf16[512,1024]{1,0:T(8,128)(2,1)S(1)}, u32[]{:S(2)}, u32[]{:S(2)}) collective-permute-start(bf16[512,1024]{1,0:T(8,128)(2,1)S(1)} %dynamic-slice_bitcast_fusion), channel_id=1, source_target_pairs={{0,1},{1,0},{2,3},{3,2},{4,5},{5,4},{6,7},{7,6},{8,9},{9,8},{10,11... | collective-permute-start | bytes 3145736 | tf_op jit(solution)/shard_map/ppermute | solution.py:24
  226.7 11.9 %collective-permute-start.9 = (bf16[256,1024]{1,0:T(8,128)(2,1)S(1)}, bf16[256,1024]{1,0:T(8,128)(2,1)S(1)}, u32[]{:S(2)}, u32[]{:S(2)}) collective-permute-start(bf16[256,1024]{1,0:T(8,128)(2,1)S(1)} %fusion.15), channel_id=1, source_target_pairs={{0,2},{1,3},{2,0},{3,1},{4,6},{5,7},{6,4},{7,5},{8,10},{9,11},{10,... | collective-permute-start | bytes 1572872 | tf_op jit(solution)/shard_map/ppermute | solution.py:24
  238.7 9.2 %collective-permute-start.10 = (bf16[256,1024]{1,0:T(8,128)(2,1)S(1)}, bf16[256,1024]{1,0:T(8,128)(2,1)S(1)}, u32[]{:S(2)}, u32[]{:S(2)}) collective-permute-start(bf16[256,1024]{1,0:T(8,128)(2,1)S(1)} %fusion.10), channel_id=1, source_target_pairs={{0,2},{1,3},{2,0},{3,1},{4,6},{5,7},{6,4},{7,5},{8,10},{9,11},{10,... | collective-permute-start | bytes 1572872 | tf_op jit(solution)/shard_map/ppermute | solution.py:24
  248.1 14.9 %collective-permute-start.11 = (bf16[512,1024]{1,0:T(8,128)(2,1)S(1)}, bf16[512,1024]{1,0:T(8,128)(2,1)S(1)}, u32[]{:S(2)}, u32[]{:S(2)}) collective-permute-start(bf16[512,1024]{1,0:T(8,128)(2,1)S(1)} %pad_maximum_fusion.2), channel_id=1, source_target_pairs={{0,1},{1,0},{2,3},{3,2},{4,5},{5,4},{6,7},{7,6},{8,9},{9,8},{10,11... | collective-permute-start | bytes 3145736 | tf_op jit(solution)/shard_map/ppermute | solution.py:24
  277.1 4.3 %copy-start.3 = (s32[1,2]{1,0:T(1,128)S(1)}, s32[1,2]{1,0:T(1,128)}, u32[]{:S(2)}) copy-start(s32[1,2]{1,0:T(1,128)} %param.5) | copy-start | bytes 28
  277.8 33.3 %all-to-all-start.1 = ((bf16[8,1,112,1024]{3,2,1,0:T(8,128)(2,1)}), bf16[8,1,112,1024]{3,2,1,0:T(8,128)(2,1)S(1)}, u32[]{:S(2)}, u32[]{:S(2)}) async-start(bf16[8,1,112,1024]{3,2,1,0:T(8,128)(2,1)} %fusion.16), calls=%async_computation.1 | async-start | bytes 3670016 | tf_op jit(solution)/shard_map/all_to_all | solution.py:90
